TPU v7x, 32 devices: a whole 2x2x4 slice. The times are simulated.
32 devices in a mesh: dp: 4 (over y, core), seq: 8 (over z, x).
Axes of the slice: x: 2, y: 2, z: 4, core: 2. Of those that a mesh axis runs over, the one named last changes fastest.
Arguments:
- queries: bfloat16 [4, 1024, 2048], P('dp', 'seq'), may hold values from -12 to 12
- keys: bfloat16 [4, 1024, 512], P('dp', 'seq'), may hold values from -4 to 4
- values: bfloat16 [4, 1024, 512], P('dp', 'seq'), may hold values from -6 to 6
- segments: int32 [4, 1024], P('dp', 'seq'), may hold values from 0 to 3, never falling along the last dimension, each value on 1 to 896 neighbouring positions
- task_ids: int32 [4], replicated, may hold values from 0 to 15
- prompt_keys: bfloat16 [16, 128, 512], P('seq'), may hold values from -4 to 4
- prompt_values: bfloat16 [16, 128, 512], P('seq'), may hold values from -6 to 6
- grad_out: bfloat16 [4, 1024, 2048], P('dp', 'seq'), may hold values from -6 to 6
Outputs:
- attended: bfloat16 [4, 1024, 2048], P('dp', 'seq')
- prompt_key_grad: float32 [16, 128, 512], P('seq')
- prompt_value_grad: float32 [16, 128, 512], P('seq')
Inputs may be any that keep to these rules, and one draw needn't show every extreme that they name: `segments`: along each example the document numbers never fall; one document holds 896 tokens.
All inputs are finite; a program needn't handle non-finite values.
Results may differ from a plain program's by a relative error of at most 0.0096.
Values may be sent and summed in bfloat16 or wider, within the bound.
A program may use at most 128 MiB of HBM per device.

v0:
```python
import math
import jax
import jax.numpy as jnp
from jax import lax
from jax.sharding import PartitionSpec as P

KVH = 4
GROUP = 4
HD = 128
PROMPT = 128


def spread(value, axis, source):
    kept = jnp.where(lax.axis_index(axis) == source, value, 0).astype(value.dtype)
    return lax.psum(kept, axis)


def shards(queries, keys, values, segments, task_ids, prompt_keys, prompt_values, grad_out):
    tok_rows = queries.shape[1]
    scaling = 1.0 / math.sqrt(HD)
    seq_rank = lax.axis_index("seq")
    query_heads = queries[0].reshape(tok_rows, KVH, GROUP, HD)
    query_segments = segments[0]
    query_index = seq_rank * tok_rows + lax.iota(jnp.int32, tok_rows)
    all_segments = lax.all_gather(segments[0], "seq", axis=0, tiled=True)
    bank_size = prompt_keys.shape[0]
    my_task = task_ids[lax.axis_index("dp")]
    prompt_owner = my_task // bank_size
    bank_slot = my_task % bank_size
    local_pair = jnp.stack(
        [
            lax.dynamic_index_in_dim(prompt_keys, bank_slot, 0, keepdims=False),
            lax.dynamic_index_in_dim(prompt_values, bank_slot, 0, keepdims=False),
        ]
    )
    shared_pair = spread(local_pair, "seq", prompt_owner)
    prompt_key_heads = shared_pair[0].reshape(PROMPT, KVH, HD)
    prompt_value_heads = shared_pair[1].reshape(PROMPT, KVH, HD)
    prompt_scores = (
        jnp.einsum(
            "tkgd,pkd->tkgp", query_heads, prompt_key_heads, preferred_element_type=jnp.float32
        )
        * scaling
    )
    maximum = jnp.max(prompt_scores, axis=-1)
    weights = jnp.exp(prompt_scores - maximum[..., None])
    totals = jnp.sum(weights, axis=-1)
    accumulated = jnp.einsum(
        "tkgp,pkd->tkgd",
        weights.astype(jnp.bfloat16),
        prompt_value_heads,
        preferred_element_type=jnp.float32,
    )
    carried = (maximum, totals, accumulated)

    def absorb_rows(state_now, stacked, first_row):
        key_count = stacked.shape[1]
        key_index = first_row + lax.iota(jnp.int32, key_count)
        key_segments = lax.dynamic_slice_in_dim(
            all_segments, jnp.maximum(first_row, 0), key_count, 0
        )
        key_mask = (
            (key_segments[None, :] == query_segments[:, None])
            & (key_index[None, :] <= query_index[:, None])
            & True
        )

        def update(inner_state):
            old_peak, old_totals, old_accum = inner_state
            key_heads = stacked[0].reshape(key_count, KVH, HD)
            value_heads = stacked[1].reshape(key_count, KVH, HD)
            scores = (
                jnp.einsum(
                    "tkgd,skd->tkgs", query_heads, key_heads, preferred_element_type=jnp.float32
                )
                * scaling
            )
            mask_wide = key_mask[:, None, None, :]
            new_peak = jnp.maximum(
                old_peak, jnp.max(jnp.where(mask_wide, scores, -jnp.inf), axis=-1)
            )
            shrink = jnp.exp(old_peak - new_peak)
            block_weights = jnp.where(mask_wide, jnp.exp(scores - new_peak[..., None]), 0.0)
            new_totals = old_totals * shrink + jnp.sum(block_weights, axis=-1)
            new_accum = old_accum * shrink[..., None] + jnp.einsum(
                "tkgs,skd->tkgd",
                block_weights.astype(jnp.bfloat16),
                value_heads,
                preferred_element_type=jnp.float32,
            )
            return (new_peak, new_totals, new_accum)

        return lax.cond(jnp.any(key_mask), update, lambda inner_state: inner_state, state_now)

    own_pair = jnp.stack([keys[0], values[0]])
    stacked = lax.all_gather(own_pair, "seq", axis=1, tiled=True)
    key_count = stacked.shape[1]
    tile_rows = 512

    def loop_tile(block_index, inner_state):
        offset = block_index * tile_rows
        piece = lax.dynamic_slice_in_dim(stacked, offset, tile_rows, 1)
        return absorb_rows(inner_state, piece, offset)

    carried = lax.fori_loop(0, key_count // tile_rows, loop_tile, carried)
    maximum, totals, accumulated = carried
    attended = (accumulated / totals[..., None]).astype(jnp.bfloat16)
    log_norm = maximum + jnp.log(totals)
    grad_heads = grad_out[0].reshape(tok_rows, KVH, GROUP, HD)
    attended_wide = lax.optimization_barrier(attended).astype(jnp.float32)
    row_delta = jnp.sum(grad_heads.astype(jnp.float32) * attended_wide, axis=-1)
    prompt_probs = jnp.exp(prompt_scores - log_norm[..., None])
    prompt_dots = jnp.einsum(
        "tkgd,pkd->tkgp", grad_heads, prompt_value_heads, preferred_element_type=jnp.float32
    )
    score_grad = prompt_probs * (prompt_dots - row_delta[..., None])
    value_part = jnp.einsum(
        "tkgp,tkgd->pkd",
        prompt_probs.astype(jnp.bfloat16),
        grad_heads,
        preferred_element_type=jnp.float32,
    )
    key_part = (
        jnp.einsum(
            "tkgp,tkgd->pkd",
            score_grad.astype(jnp.bfloat16),
            query_heads,
            preferred_element_type=jnp.float32,
        )
        * scaling
    )
    value_part = value_part.reshape(PROMPT, KVH * HD)
    key_part = key_part.reshape(PROMPT, KVH * HD)
    key_sum, value_sum = lax.psum((key_part, value_part), "seq")
    key_all, value_all = (
        lax.all_gather(key_sum[None].astype(jnp.bfloat16), "dp", axis=0, tiled=True).astype(
            jnp.float32
        ),
        lax.all_gather(value_sum[None].astype(jnp.bfloat16), "dp", axis=0, tiled=True).astype(
            jnp.float32
        ),
    )
    own_tasks = seq_rank * bank_size + lax.iota(jnp.int32, bank_size)
    matches = (task_ids[:, None] == own_tasks[None, :])[:, :, None, None]
    key_grad = jnp.sum(jnp.where(matches, key_all[:, None], 0.0), axis=0)
    value_grad = jnp.sum(jnp.where(matches, value_all[:, None], 0.0), axis=0)
    return (attended.reshape(1, tok_rows, KVH * GROUP * HD), key_grad, value_grad)


def solution(mesh):
    in_specs = (
        P("dp", "seq", None),
        P("dp", "seq", None),
        P("dp", "seq", None),
        P("dp", "seq"),
        P(),
        P("seq", None, None),
        P("seq", None, None),
        P("dp", "seq", None),
    )
    out_specs = (P("dp", "seq", None), P("seq", None, None), P("seq", None, None))
    return jax.shard_map(shards, mesh=mesh, in_specs=in_specs, out_specs=out_specs, check_vma=False)
```

profile of v0, /device:TPU:0, one launch (start us, length us, event | category | flops | bytes accessed | tf_op | source)
XLA Modules:
  0.0 223.2 jit_solution(11185119642300208240)
XLA Ops:
  7.2 0.0 copy-start.4
  7.2 0.0 copy-start.2
  7.2 0.0 copy-start.3
  7.2 0.0 all-reduce.4.cloned.1.call-start
  7.2 1.3 dynamic_slice.28
  11.1 1.0 constant_dynamic-slice_fusion.2
  12.1 0.1 copy.88
  12.3 0.1 copy.87
  12.4 0.7 maximum_select_fusion
  13.2 0.0 all-reduce.4.cloned.1.call-update
  13.2 0.0 all-gather.5.cloned.1.call-start
  13.2 1.0 copy.52
  14.3 1.0 copy.51
  15.3 0.7 pad_maximum_fusion
  16.0 0.0 all-gather.5.cloned.1.call-update
  16.0 1.3 copy.47
  17.4 0.3 copy.54
  17.7 0.0 copy-done.2
  17.7 0.3 copy.56
  17.9 0.0 copy-done.3
  17.9 22.3 %all-gather = s32[1,1024]{1,0:T(1,128)S(1)} all-gather(s32[1,128]{1,0:T(1,128)S(1)} %copy-done.3), channel_id=2, replica_groups=mesh['dp'=4,'seq'=8] {'seq'}, dimensions={1}, use_global_device_ids=true | all-gather | bytes 4608 | tf_op jit(solution)/shard_map/all_gather | solution.py:25
  40.2 0.0 copy-done.4
  40.2 0.1 broadcast_compare_fusion
  40.3 46.8 %all-reduce.4.cloned.1.call-done = bf16[2,128,512]{1,2,0:T(8,128)(2,1)} async-done(((bf16[2,128,512]{1,2,0:T(8,128)(2,1)}), bf16[2,128,512]{1,2,0:T(8,128)(2,1)}) %all-reduce.4.cloned.1.call-update) | async-done | bytes 262160 | tf_op jit(solution)/shard_map/psum | solution.py:15
  87.1 1.0 fusion.39
  88.1 0.4 fusion.40
  88.4 1.3 convolution_bitcast_fusion.1
  89.7 2.5 %copy.53 = f32[128,4,4,128]{3,0,2,1:T(8,128)} copy(f32[128,4,4,128]{0,3,2,1:T(8,128)} %convolution_bitcast_fusion.1) | data formatting | bytes 2097152
  92.3 0.2 fusion.29
  92.5 46.8 %all-gather.5.cloned.1.call-done = bf16[2,1024,512]{1,2,0:T(8,128)(2,1)} async-done(((bf16[2,128,512]{1,2,0:T(8,128)(2,1)}), bf16[2,1024,512]{1,2,0:T(8,128)(2,1)}) %all-gather.5.cloned.1.call-update) | async-done | bytes 2097168 | tf_op jit(solution)/shard_map/all_gather | solution.py:96
  139.3 8.8 %while.18 = (s32[]{:T(128)}, f32[128,4,4]{0,2,1:T(4,128)S(1)}, f32[128,4,4]{0,2,1:T(4,128)S(1)}, f32[128,4,4,128]{3,0,2,1:T(8,128)}, s32[1024]{0:T(1024)S(1)}, /...) while((s32[]{:T(128)}, f32[128,4,4]{0,2,1:T(4,128)S(1)}, ...), condition=%wide.region_9.10_spmd.clone, body=%wide.region_3.9_spmd.clone.sunk | while | flops 549196416 | bytes 27144068 | solution.py:105
  139.3 0.1 dynamic_slice.35
  139.4 0.8 fusion.52
  140.8 5.6 %conditional.3 = ((f32[128,4,4]{0,2,1:T(4,128)S(1)}, f32[128,4,4]{0,2,1:T(4,128)S(1)}, f32[128,4,4,128]{3,0,2,1:T(8,128)})) conditional(s32[]{:T(128)} %convert_element_type.85, (f32[128,4,4]{0,2,1:T(4,128)S(1)}, f32[128,4,4]{0,2,1:T(4,128)S(1)}, f32[128,4,4,128]{3,0,2,1:T(8,128)}) %tuple.65, (pred[128,512]{0,1:T(8,128)(4,1)S(1)}, s32[]{:T(128)}, ...), branch_computations={%region_5.5_spmd, %region_6.8_spmd} | conditional | flops 548933632 | bytes 27066510 | solution.py:93
  140.9 1.3 constant_dynamic-slice_fusion.1
  142.1 0.0 copy-start
  142.2 0.9 fusion.2
  143.0 0.9 fusion.6
  143.9 0.0 copy-done
  143.9 1.5 fusion.16
  145.4 0.0 copy-start.1
  145.5 1.0 copy-done.1
  146.4 0.1 dynamic_slice.35
  146.5 0.8 fusion.52
  148.0 2.6 %copy.55 = f32[128,4,4,128]{0,3,2,1:T(8,128)} copy(f32[128,4,4,128]{3,0,2,1:T(8,128)} %get-tuple-element.225) | data formatting | bytes 2097152 | tf_op jit(solution)/shard_map/while | solution.py:105
  150.6 1.3 divide_convert_fusion
  151.9 1.0 copy.63
  153.0 0.2 multiply_reduce_fusion
  153.1 0.3 fusion.31
  153.4 0.6 fusion.27
  154.0 45.7 %all-reduce.5 = (bf16[128,512]{0,1:T(8,128)(2,1)S(1)}, bf16[128,512]{0,1:T(8,128)(2,1)S(1)}) all-reduce(f32[128,512]{0,1:T(8,128)S(1)} %bitcast.123, f32[128,512]{0,1:T(8,128)S(1)} %bitcast.122), channel_id=1, replica_groups=mesh['dp'=4,'seq'=8] {'seq'}, use_global_device_ids=true, to_apply=%region_11.12 | all-reduce | flops 131072 | bytes 786432 | tf_op jit(solution)/shard_map/psum | solution.py:134
  199.7 7.6 %all-gather.2 = bf16[512,512]{0,1:T(8,128)(2,1)S(1)} all-gather(bf16[128,512]{0,1:T(8,128)(2,1)S(1)} %get-tuple-element.306), channel_id=4, replica_groups=mesh['dp'=4,'seq'=8] {'dp'}, dimensions={0}, use_global_device_ids=true | all-gather | bytes 655360 | tf_op jit(solution)/shard_map/all_gather | solution.py:139
  207.3 0.2 copy.86
  207.5 7.3 %all-gather.1 = bf16[512,512]{0,1:T(8,128)(2,1)S(1)} all-gather(bf16[128,512]{0,1:T(8,128)(2,1)S(1)} %get-tuple-element.305), channel_id=3, replica_groups=mesh['dp'=4,'seq'=8] {'dp'}, dimensions={0}, use_global_device_ids=true | all-gather | bytes 655360 | tf_op jit(solution)/shard_map/all_gather | solution.py:136
  214.8 0.2 copy.85
  215.0 1.3 select_reduce_fusion
  (10 shorter events, 0.1 us)
Async XLA Ops:
  7.2 33.1 %copy-start.4 = (s32[4]{0:T(128)S(1)}, s32[4]{0:T(128)}, u32[]{:S(2)}) copy-start(s32[4]{0:T(128)} %param.16) | copy-start | bytes 52
  7.2 10.5 %copy-start.2 = (bf16[1,128,2048]{2,1,0:T(8,128)(2,1)S(1)}, bf16[1,128,2048]{2,1,0:T(8,128)(2,1)}, u32[]{:S(2)}) copy-start(bf16[1,128,2048]{2,1,0:T(8,128)(2,1)} %param.19) | copy-start | bytes 1572868
  7.2 10.8 %copy-start.3 = (s32[1,128]{1,0:T(1,128)S(1)}, s32[1,128]{1,0:T(1,128)}, u32[]{:S(2)}) copy-start(s32[1,128]{1,0:T(1,128)} %param.15) | copy-start | bytes 1540
  7.2 79.9 %all-reduce.4.cloned.1.call-start = ((), (), s32[]{:S(2)}) async-start(), calls=%async_computation | async-start | bytes 524288 | tf_op jit(solution)/shard_map/psum | solution.py:15
  13.2 126.1 %all-gather.5.cloned.1.call-start = ((), (), s32[]{:S(2)}) async-start(), calls=%async_computation.1 | async-start | bytes 2359296 | tf_op jit(solution)/shard_map/all_gather | solution.py:96
  142.1 1.8 copy-start
  145.4 1.0 copy-start.1
Sparse Core Ops, SparseCore 0:
  13.3 73.7 all-reduce.3
  89.7 49.5 all-gather.4
where the time goes:
time: 224 us; the launch traced here: 223 us
  waiting for transfers between devices  93.6 us (42%)
  blocking collectives  82.9 us (37%)
  between operations  16.8 us (8%)
  local copies, waits for them, and re-layouts  16.4 us (7%)
  other arithmetic  7.1 us (3%)
  matrix products  4.91 us (2%)
    all_gather x1, waiting for transfers between devices, shards(): stacked = lax.all_gather(own_pair, 'seq', axis=1, tiled=True)  46.8 us
    psum x1, waiting for transfers between devices, spread(): return lax.psum(kept, axis)  46.8 us
    psum x1, blocking collectives, shards(): key_sum, value_sum = lax.psum((key_part, value_part), 'seq')  45.7 us
    all_gather x1, blocking collectives, shards(): all_segments = lax.all_gather(segments[0], 'seq', axis=0, tiled=True)  22.3 us
    unnamed x15, local copies, waits for them, and re-layouts  7.72 us
    all_gather x1, blocking collectives, shards(): lax.all_gather(value_sum[None].astype(jnp.bfloat16), 'dp', axis=0, tiled=...  7.59 us
    all_gather x1, blocking collectives, shards(): lax.all_gather(key_sum[None].astype(jnp.bfloat16), 'dp', axis=0, tiled=True)  7.3 us
  transfers between devices with their start and end apart: 2, of which 2 were waited for; matrix products, arithmetic and copies ran while one was open for 5% of the time, Pallas kernels for 0%

commit v1 on v0

--- a/solution.py
+++ b/solution.py
@@ -12,7 +12,10 @@
 
 def spread(value, axis, source):
     kept = jnp.where(lax.axis_index(axis) == source, value, 0).astype(value.dtype)
-    return lax.psum(kept, axis)
+    cut_frame_by_axis = lambda peer_axis, mine: jnp.sum(
+        lax.all_gather(mine, axis_name=peer_axis), 0
+    )
+    return cut_frame_by_axis(axis, kept)
 
 
 def shards(queries, keys, values, segments, task_ids, prompt_keys, prompt_values, grad_out):

time: 224 us -> 201 us (0.90)
  waiting for transfers between devices: 93.6 us -> 69.7 us
    psum x1 -> x0, waiting for transfers between devices: 46.8 us -> none  [spread(): return lax.psum(kept, axis)]
    all_gather x0 -> x1, waiting for transfers between devices: none -> 24.8 us  [spread(): lax.all_gather(mine, axis_name=peer_axis)]
    unnamed x15 -> x13, local copies, waits for them, and re-layouts: 7.72 us -> 7.49 us
  transfers between devices with their start and end apart: 2 -> 2, of which waited for: 2 -> 2; matrix products, arithmetic and copies ran while one was open for 5% -> 6% of each run, Pallas kernels for 0% -> 0%
where the time goes in v1:
time: 201 us; the launch traced here: 200 us
  blocking collectives  83 us (41%)
  waiting for transfers between devices  69.7 us (35%)
  between operations  16.8 us (8%)
  local copies, waits for them, and re-layouts  15.4 us (8%)
  other arithmetic  9.06 us (5%)
  matrix products  4.92 us (2%)
    psum x1, blocking collectives, shards(): key_sum, value_sum = lax.psum((key_part, value_part), 'seq')  45.7 us
    all_gather x1, waiting for transfers between devices, shards(): stacked = lax.all_gather(own_pair, 'seq', axis=1, tiled=True)  44.9 us
    all_gather x1, waiting for transfers between devices, spread(): lax.all_gather(mine, axis_name=peer_axis)  24.8 us
    all_gather x1, blocking collectives, shards(): all_segments = lax.all_gather(segments[0], 'seq', axis=0, tiled=True)  22.4 us
    all_gather x1, blocking collectives, shards(): lax.all_gather(value_sum[None].astype(jnp.bfloat16), 'dp', axis=0, tiled=...  7.59 us
    unnamed x13, local copies, waits for them, and re-layouts  7.49 us
    all_gather x1, blocking collectives, shards(): lax.all_gather(key_sum[None].astype(jnp.bfloat16), 'dp', axis=0, tiled=True)  7.3 us
  transfers between devices with their start and end apart: 2, of which 2 were waited for; matrix products, arithmetic and copies ran while one was open for 6% of the time, Pallas kernels for 0%

profile of v1, /device:TPU:0, one launch (start us, length us, event | category | flops | bytes accessed | tf_op | source)
XLA Modules:
  0.0 200.4 jit_solution(16342345893021731642)
XLA Ops:
  7.2 0.0 copy-start.4
  7.2 0.0 copy-start.2
  7.2 0.0 copy-start.3
  7.2 0.0 all-gather.6.cloned.1.call-start
  7.2 1.3 dynamic_slice.28
  11.2 1.0 dynamic-slice_bitcast_fusion
  12.2 0.7 maximum_select_fusion
  12.9 0.0 all-gather.6.cloned.1.call-update
  12.9 0.0 all-gather.8.cloned.1.call-start
  13.0 1.0 copy.71
  14.0 1.0 copy.70
  15.0 0.7 pad_maximum_fusion
  15.8 0.0 all-gather.8.cloned.1.call-update
  15.8 1.3 copy.65
  17.1 0.3 copy.73
  17.4 0.0 copy-done.2
  17.4 0.3 copy.75
  17.7 0.0 copy-done.3
  17.7 22.4 %all-gather = s32[1,1024]{1,0:T(1,128)S(1)} all-gather(s32[1,128]{1,0:T(1,128)S(1)} %copy-done.3), channel_id=2, replica_groups=mesh['dp'=4,'seq'=8] {'seq'}, dimensions={1}, use_global_device_ids=true | all-gather | bytes 4608 | tf_op jit(solution)/shard_map/all_gather | solution.py:28
  40.1 0.0 copy-done.4
  40.1 0.1 broadcast_compare_fusion
  40.2 24.8 %all-gather.6.cloned.1.call-done = bf16[8,2,128,512]{3,2,1,0:T(8,128)(2,1)} async-done(((bf16[1,2,128,512]{3,2,1,0:T(8,128)(2,1)}), bf16[8,2,128,512]{3,2,1,0:T(8,128)(2,1)}) %all-gather.6.cloned.1.call-update) | async-done | bytes 2097168 | tf_op jit(solution)/shard_map/all_gather | solution.py:16
  64.9 2.0 reduce_sum.58
  66.9 0.1 copy.64
  67.0 0.1 copy.68
  67.2 0.4 fusion.40
  67.6 1.3 convolution_bitcast_fusion.1
  68.9 2.5 %copy.72 = f32[128,4,4,128]{3,0,2,1:T(8,128)} copy(f32[128,4,4,128]{0,3,2,1:T(8,128)} %convolution_bitcast_fusion.1) | data formatting | bytes 2097152
  71.4 0.2 fusion.29
  71.6 44.9 %all-gather.8.cloned.1.call-done = bf16[2,1024,512]{1,2,0:T(8,128)(2,1)} async-done(((bf16[2,128,512]{1,2,0:T(8,128)(2,1)}), bf16[2,1024,512]{1,2,0:T(8,128)(2,1)}) %all-gather.8.cloned.1.call-update) | async-done | bytes 2097168 | tf_op jit(solution)/shard_map/all_gather | solution.py:99
  116.5 8.8 %while.18 = (s32[]{:T(128)}, f32[128,4,4]{0,2,1:T(4,128)S(1)}, f32[128,4,4]{0,2,1:T(4,128)S(1)}, f32[128,4,4,128]{3,0,2,1:T(8,128)}, s32[1024]{0:T(1024)S(1)}, /...) while((s32[]{:T(128)}, f32[128,4,4]{0,2,1:T(4,128)S(1)}, ...), condition=%wide.region_9.10_spmd.clone, body=%wide.region_3.9_spmd.clone.sunk | while | flops 549196416 | bytes 27144068 | solution.py:108
  116.5 0.1 dynamic_slice.35
  116.5 0.8 fusion.52
  118.0 5.6 %conditional.3 = ((f32[128,4,4]{0,2,1:T(4,128)S(1)}, f32[128,4,4]{0,2,1:T(4,128)S(1)}, f32[128,4,4,128]{3,0,2,1:T(8,128)})) conditional(s32[]{:T(128)} %convert_element_type.87, (f32[128,4,4]{0,2,1:T(4,128)S(1)}, f32[128,4,4]{0,2,1:T(4,128)S(1)}, f32[128,4,4,128]{3,0,2,1:T(8,128)}) %tuple.67, (pred[128,512]{0,1:T(8,128)(4,1)S(1)}, s32[]{:T(128)}, ...), branch_computations={%region_5.5_spmd, %region_6.8_spmd} | conditional | flops 548933632 | bytes 27066510 | solution.py:96
  118.1 1.3 constant_dynamic-slice_fusion.1
  119.3 0.0 copy-start
  119.3 0.9 fusion.2
  120.2 0.9 fusion.6
  121.1 0.0 copy-done
  121.1 1.5 fusion.16
  122.6 0.0 copy-start.1
  122.6 1.0 copy-done.1
  123.6 0.1 dynamic_slice.35
  123.7 0.8 fusion.52
  125.2 2.6 %copy.74 = f32[128,4,4,128]{0,3,2,1:T(8,128)} copy(f32[128,4,4,128]{3,0,2,1:T(8,128)} %get-tuple-element.225) | data formatting | bytes 2097152 | tf_op jit(solution)/shard_map/while | solution.py:108
  127.8 1.3 divide_convert_fusion
  129.1 1.0 copy.82
  130.1 0.2 multiply_reduce_fusion
  130.3 0.3 fusion.31
  130.6 0.6 fusion.27
  131.2 45.7 %all-reduce.2 = (bf16[128,512]{0,1:T(8,128)(2,1)S(1)}, bf16[128,512]{0,1:T(8,128)(2,1)S(1)}) all-reduce(f32[128,512]{0,1:T(8,128)S(1)} %bitcast.127, f32[128,512]{0,1:T(8,128)S(1)} %bitcast.126), channel_id=1, replica_groups=mesh['dp'=4,'seq'=8] {'seq'}, use_global_device_ids=true, to_apply=%region_11.12 | all-reduce | flops 131072 | bytes 786432 | tf_op jit(solution)/shard_map/psum | solution.py:137
  176.9 7.6 %all-gather.2 = bf16[512,512]{0,1:T(8,128)(2,1)S(1)} all-gather(bf16[128,512]{0,1:T(8,128)(2,1)S(1)} %get-tuple-element.318), channel_id=4, replica_groups=mesh['dp'=4,'seq'=8] {'dp'}, dimensions={0}, use_global_device_ids=true | all-gather | bytes 655360 | tf_op jit(solution)/shard_map/all_gather | solution.py:142
  184.5 0.2 copy.105
  184.7 7.3 %all-gather.1 = bf16[512,512]{0,1:T(8,128)(2,1)S(1)} all-gather(bf16[128,512]{0,1:T(8,128)(2,1)S(1)} %get-tuple-element.317), channel_id=3, replica_groups=mesh['dp'=4,'seq'=8] {'dp'}, dimensions={0}, use_global_device_ids=true | all-gather | bytes 655360 | tf_op jit(solution)/shard_map/all_gather | solution.py:139
  192.0 0.2 copy.104
  192.2 1.3 select_reduce_fusion
  (11 shorter events, 0.1 us)
Async XLA Ops:
  7.2 32.9 %copy-start.4 = (s32[4]{0:T(128)S(1)}, s32[4]{0:T(128)}, u32[]{:S(2)}) copy-start(s32[4]{0:T(128)} %param.16) | copy-start | bytes 52
  7.2 10.2 %copy-start.2 = (bf16[1,128,2048]{2,1,0:T(8,128)(2,1)S(1)}, bf16[1,128,2048]{2,1,0:T(8,128)(2,1)}, u32[]{:S(2)}) copy-start(bf16[1,128,2048]{2,1,0:T(8,128)(2,1)} %param.19) | copy-start | bytes 1572868
  7.2 10.5 %copy-start.3 = (s32[1,128]{1,0:T(1,128)S(1)}, s32[1,128]{1,0:T(1,128)}, u32[]{:S(2)}) copy-start(s32[1,128]{1,0:T(1,128)} %param.15) | copy-start | bytes 1540
  7.2 57.7 %all-gather.6.cloned.1.call-start = ((), (), s32[]{:S(2)}) async-start(), calls=%async_computation | async-start | bytes 2359296 | tf_op jit(solution)/shard_map/all_gather | solution.py:16
  12.9 103.5 %all-gather.8.cloned.1.call-start = ((), (), s32[]{:S(2)}) async-start(), calls=%async_computation.1 | async-start | bytes 2359296 | tf_op jit(solution)/shard_map/all_gather | solution.py:99
  119.3 1.8 copy-start
  122.6 1.0 copy-start.1
Sparse Core Ops, SparseCore 0:
  13.0 51.8 all-gather.5
  67.5 48.8 all-gather.7
